TPU v7x, 32 devices: a whole 2x2x4 slice. The times are simulated.
32 devices in a mesh: section: 2 (over core), seq: 4 (over y, x), head: 4 (over z).
Axes of the slice: x: 2, y: 2, z: 4, core: 2. Of those that a mesh axis runs over, the one named last changes fastest.
Arguments:
- x_in: bfloat16 [2, 1024, 8192], P('section', 'seq', 'head'), may hold values from -6 to 6
- b_in: bfloat16 [2, 1024, 2048], P('section', 'seq', 'head'), may hold values from -6 to 6
- c_in: bfloat16 [2, 1024, 2048], P('section', 'seq', 'head'), may hold values from -6 to 6
- z_in: bfloat16 [2, 1024, 8192], P('section', 'seq', 'head'), may hold values from -6 to 6
- dt_raw: float32 [2, 128, 1024], P('section', 'head', 'seq'), may hold values from -5 to 5
- conv_x: float32 [2, 4, 8192], P('section', None, 'head'), may hold values from -3 to 3
- conv_b: float32 [2, 4, 2048], P('section', None, 'head'), may hold values from -3 to 3
- conv_c: float32 [2, 4, 2048], P('section', None, 'head'), may hold values from -3 to 3
- a_rate: float32 [2, 128], P('section', 'head'), may hold values from 0.0001 to 1
- dt_bias: float32 [2, 128], P('section', 'head'), may hold values from -3 to -0.5
- skip_d: float32 [2, 128], P('section', 'head'), may hold values from 0.5 to 2
- norm_gain: float32 [2, 8192], P('section', 'head'), may hold values from 0.25 to 1.75
- out_weight: bfloat16 [2, 8192, 8192], P('section', 'head', 'seq'), may hold values from -0.0625 to 0.0625
Outputs:
- mixed: bfloat16 [2, 1024, 8192], P('section', ('seq', 'head'))
All inputs are finite; a program needn't handle non-finite values.
Results may differ from a plain program's by a relative error of at most 0.007.
Values may be sent and summed in bfloat16 or wider, within the bound.
A program may use at most 128 MiB of HBM per device.

v0:
```python
import jax
import jax.numpy as jnp
from jax import lax
from jax.sharding import PartitionSpec as P

N = 256
epsilon = 1e-05


def passed_along(block, axis, distance):
    devices = range(lax.axis_size(axis))
    route = [(i - distance, i) for i in devices if i - distance in devices]
    return lax.ppermute(block, axis, route)


def entering(decay, block, axis):
    size, place = (lax.axis_size(axis), lax.axis_index(axis))
    decays = lax.all_gather(decay, axis)
    blocks = lax.all_gather(block.astype(jnp.bfloat16), axis)
    carried = jnp.zeros_like(block)
    for k in range(size - 1):
        after = decays[k][:, :, None, None] * carried + blocks[k].astype(jnp.float32)
        carried = jnp.where(k < place, after, carried)
    return carried


def passed_along_2(block, axis, distance):
    devices = range(lax.axis_size(axis))
    route = [((i - distance) % len(devices), i) for i in devices]
    return lax.ppermute(block, axis, route)


def conv_silu(padded, kernel, length):
    kernel_taps = kernel.shape[0]
    summed = jnp.zeros((length, padded.shape[1]), jnp.float32)
    for offset in range(kernel_taps):
        summed = summed + kernel[offset] * padded[offset : offset + length].astype(jnp.float32)
    return jax.nn.silu(summed).astype(jnp.bfloat16)


def per_device(
    x_in,
    b_in,
    c_in,
    z_in,
    dt_raw,
    conv_x,
    conv_b,
    conv_c,
    a_rate,
    dt_bias,
    skip_d,
    norm_gain,
    out_weight,
):
    x_local = x_in[0]
    b_local = b_in[0]
    c_local = c_in[0]
    length = x_local.shape[0]
    kernel_taps = conv_x.shape[1]
    x_cols = x_local.shape[1]
    b_cols = b_local.shape[1]
    edge_rows = jnp.concatenate(
        [
            x_local[length - kernel_taps + 1 :],
            b_local[length - kernel_taps + 1 :],
            c_local[length - kernel_taps + 1 :],
        ],
        axis=1,
    )
    before = passed_along(edge_rows, "seq", 1)
    x_conv = conv_silu(jnp.concatenate([before[:, :x_cols], x_local], axis=0), conv_x[0], length)
    b_conv = conv_silu(
        jnp.concatenate([before[:, x_cols : x_cols + b_cols], b_local], axis=0), conv_b[0], length
    )
    c_conv = conv_silu(
        jnp.concatenate([before[:, x_cols + b_cols :], c_local], axis=0), conv_c[0], length
    )
    head_count = dt_raw.shape[1]
    group_count = b_cols // N
    per_group = head_count // group_count
    head_dim = x_cols // head_count
    step_size = jax.nn.softplus(dt_raw[0] + dt_bias[0][:, None])
    log_decay = jnp.cumsum(-a_rate[0][:, None] * step_size, axis=1)
    x_groups = x_conv.reshape(length, group_count, per_group, head_dim)
    b_groups = b_conv.reshape(length, group_count, N)
    c_groups = c_conv.reshape(length, group_count, N)
    log_groups = log_decay.reshape(group_count, per_group, length)
    step_groups = step_size.reshape(group_count, per_group, length)
    scores = jnp.einsum("tgn,ugn->gtu", c_groups, b_groups, preferred_element_type=jnp.float32)
    causal = jnp.arange(length)[:, None] >= jnp.arange(length)[None, :]
    spread_log = log_groups[:, :, :, None] - log_groups[:, :, None, :]
    damping = jnp.where(causal, jnp.exp(jnp.minimum(spread_log, 0.0)), 0.0)
    weights = (damping * step_groups[:, :, None, :] * scores[:, None]).astype(jnp.bfloat16)
    inside = jnp.einsum("gjtu,ugjp->tgjp", weights, x_groups, preferred_element_type=jnp.float32)
    to_end = jnp.exp(log_groups[:, :, -1:] - log_groups) * step_groups
    x_weighted = (
        x_groups.astype(jnp.float32) * jnp.transpose(to_end, (2, 0, 1))[..., None]
    ).astype(jnp.bfloat16)
    block_sum = jnp.einsum(
        "ugjp,ugn->gjpn", x_weighted, b_groups, preferred_element_type=jnp.float32
    )
    block_decay = jnp.exp(log_groups[:, :, -1])
    carried = entering(block_decay, block_sum, "seq")
    carried_b = carried.astype(jnp.bfloat16)
    outside = jnp.einsum("tgn,gjpn->tgjp", c_groups, carried_b, preferred_element_type=jnp.float32)
    outside = outside * jnp.transpose(jnp.exp(log_groups), (2, 0, 1))[..., None]
    skip_term = skip_d[0].reshape(group_count, per_group)
    out_ssm = inside + outside + skip_term[None, :, :, None] * x_groups.astype(jnp.float32)
    gate_act = jax.nn.silu(z_in[0].astype(jnp.float32)).reshape(
        length, group_count, per_group * head_dim
    )
    gated = out_ssm.reshape(length, group_count, per_group * head_dim) * gate_act
    inverse_rms = lax.rsqrt(jnp.mean(gated * gated, axis=2, keepdims=True) + epsilon)
    hidden = ((gated * inverse_rms).reshape(length, x_cols) * norm_gain[0]).astype(jnp.bfloat16)
    local_weight = out_weight[0]
    terms = jnp.dot(
        lax.all_gather(hidden, "seq", axis=0, tiled=True),
        local_weight,
        preferred_element_type=jnp.float32,
    )
    shards = lax.axis_size("seq")
    terms = terms.astype(jnp.bfloat16).reshape(shards, length, local_weight.shape[1])
    summed = lax.psum_scatter(terms, "head", scatter_dimension=1, tiled=True)
    spread = lax.all_to_all(summed, "seq", split_axis=0, concat_axis=2, tiled=True)
    mixed = spread.reshape(spread.shape[1], spread.shape[2])
    passed = passed_along_2(mixed, "section", 1)
    return passed[None]


def solution(mesh):
    return jax.shard_map(
        per_device,
        mesh=mesh,
        in_specs=(
            P("section", "seq", "head"),
            P("section", "seq", "head"),
            P("section", "seq", "head"),
            P("section", "seq", "head"),
            P("section", "head", "seq"),
            P("section", None, "head"),
            P("section", None, "head"),
            P("section", None, "head"),
            P("section", "head"),
            P("section", "head"),
            P("section", "head"),
            P("section", "head"),
            P("section", "head", "seq"),
        ),
        out_specs=P("section", ("seq", "head"), None),
        check_vma=False,
    )
```

profile of v0, /device:TPU:0, one launch (start us, length us, event | category | flops | bytes accessed | tf_op | source)
XLA Modules:
  0.0 265.6 jit_solution(9218574246040160207)
XLA Ops:
  6.5 0.9 slice_bitcast_fusion
  8.1 4.9 %collective-permute-start = (bf16[3,3072]{1,0:T(4,128)(2,1)S(1)}, bf16[3,3072]{1,0:T(4,128)(2,1)S(1)}, u32[]{:S(2)}, u32[]{:S(2)}) collective-permute-start(bf16[3,3072]{1,0:T(4,128)(2,1)S(1)} %pad_maximum_fusion.3), channel_id=1, source_target_pairs={{0,4},{4,8},{8,12},{1,5},{5,9},{9,13},{2,6},{6,10},{10,14},{3,7},{... | collective-permute-start | bytes 55304 | tf_op jit(solution)/shard_map/ppermute | solution.py:13
  14.2 1.3 reduce.9
  18.2 0.9 fusion.50
  19.2 1.4 multiply_bitcast_fusion
  20.6 0.9 fusion.53
  21.4 1.9 multiply_convert_fusion.5
  23.5 1.5 multiply_convert_fusion.2
  25.5 1.4 convolution_convert_fusion
  27.8 1.6 copy.67
  29.4 8.1 %all-gather = f32[8,16,1]{1,2,0:T(1,128)S(1)} all-gather(f32[2,16,1]{1,2,0:T(1,128)S(1)} %bitcast.125), channel_id=2, replica_groups=mesh['section'=2,'seq'=4,'head'=4] {'seq'}, dimensions={0}, use_global_device_ids=true | all-gather | bytes 640 | tf_op jit(solution)/shard_map/all_gather | solution.py:18
  38.2 41.8 %all-gather.7.cloned.1.call-done = bf16[8,16,64,256]{3,2,1,0:T(8,128)(2,1)} async-done(((bf16[2,16,64,256]{3,2,1,0:T(8,128)(2,1)}), bf16[8,16,64,256]{3,2,1,0:T(8,128)(2,1)}) %all-gather.7.cloned.1.call-update) | async-done | bytes 4194320 | tf_op jit(solution)/shard_map/all_gather | solution.py:19
  80.0 3.0 %fusion.31 = f32[2,16,64,256]{3,2,1,0:T(8,128)S(1)} fusion(bf16[8,16,64,256]{3,2,1,0:T(8,128)(2,1)} %all-gather.7.cloned.1.call-done, f32[2,16]{1,0:T(2,128)S(1)} %bitcast.128, f32[2,16]{1,0:T(2,128)S(1)} %bitcast.127, f32[2,16]{1,0:T(2,128)S(1)} %bitcast.126, pred[]{:T(512)S(6)} %gt.11, pred[]{:T(512)S(6)} %gt.10, pred[]{:T(512)S(6)} %gt.9, ...), kind=kOutput, calls=%fused_computation.43 | convolution fusion | flops 274726912 | bytes 5505411 | tf_op jit(solution)/shard_map/tgn,gjpn->tgjp/dot_general | solution.py:106
  83.0 4.5 %multiply_reduce_fusion = (f32[256,2]{0,1:T(2,128)S(1)}, f32[256,2,16,64]{0,3,2,1:T(8,128)}) fusion(f32[256,2,16,64]{0,3,2,1:T(8,128)S(1)} %bitcast.99, bf16[256,2,16,64]{0,3,2,1:T(8,128)(2,1)S(1)} %bitcast.103, f32[2,16]{1,0:T(2,128)S(1)} %mul.316, f32[256,2,16]{0,2,1:T(8,128)S(1)} %copy-done.4, f32[2,16,64,256]{3,2,1,0:T(8,128)S(1)} %fusion.31, ...), kind=kOutput, calls=%fused_computation.33 | convolution fusion | flops 287309312 | bytes 8030336 | tf_op jit(solution)/shard_map/gjtu,ugjp->tgjp/dot_general | solution.py:95
  87.5 1.9 copy.66
  90.2 0.9 copy.79
  91.1 1.8 fusion.26
  92.9 52.7 %all-gather.5.cloned.1.call-done = bf16[1024,2048]{1,0:T(8,128)(2,1)} async-done(((bf16[256,2048]{1,0:T(8,128)(2,1)}), bf16[1024,2048]{1,0:T(8,128)(2,1)}) %all-gather.5.cloned.1.call-update) | async-done | bytes 4194320 | tf_op jit(solution)/shard_map/all_gather | solution.py:118
  145.6 13.8 %fusion.9 = bf16[1024,2048]{1,0:T(8,128)(2,1)} fusion(bf16[1024,2048]{1,0:T(8,128)(2,1)} %all-gather.5.cloned.1.call-done, bf16[1,2048,2048]{2,1,0:T(8,128)(2,1)} %param.25), kind=kOutput, calls=%fused_computation.10 | convolution fusion | flops 8592031744 | bytes 16777216 | tf_op jit(solution)/shard_map/dot_general | solution.py:117
  159.4 77.0 %reduce-scatter.2.cloned.1.call-done = bf16[4,64,2048]{2,1,0:T(8,128)(2,1)} async-done(((bf16[4,256,2048]{2,1,0:T(8,128)(2,1)}), bf16[4,64,2048]{2,1,0:T(8,128)(2,1)}) %reduce-scatter.2.cloned.1.call-update) | async-done | bytes 1048592 | tf_op jit(solution)/shard_map/reduce_scatter | solution.py:124
  236.4 17.6 %all_to_all.15 = bf16[4,64,2048]{2,1,0:T(8,128)(2,1)S(1)} all-to-all(bf16[4,64,2048]{2,1,0:T(8,128)(2,1)} %reduce-scatter.2.cloned.1.call-done), channel_id=1, replica_groups=mesh['section'=2,'seq'=4,'head'=4] {'seq'}, dimensions={0} | all-to-all | bytes 2097152 | tf_op jit(solution)/shard_map/all_to_all | solution.py:125
  254.0 0.8 copy.69
  255.5 2.6 collective-permute-done.1
  258.1 1.0 copy.97
  (57 shorter events, 8.3 us)
Async XLA Ops:
  6.5 16.9 %copy-start.2 = (bf16[1,256,2048]{2,1,0:T(8,128)(2,1)S(1)}, bf16[1,256,2048]{2,1,0:T(8,128)(2,1)}, u32[]{:S(2)}) copy-start(bf16[1,256,2048]{2,1,0:T(8,128)(2,1)} %param.13) | copy-start | bytes 3145732
  6.5 73.5 %all-gather.7.cloned.1.call-start = ((), (), s32[]{:S(2)}) async-start(), calls=%async_computation.4 | async-start | bytes 5242880 | tf_op jit(solution)/shard_map/all_gather | solution.py:19
  8.1 13.3 %collective-permute-start = (bf16[3,3072]{1,0:T(4,128)(2,1)S(1)}, bf16[3,3072]{1,0:T(4,128)(2,1)S(1)}, u32[]{:S(2)}, u32[]{:S(2)}) collective-permute-start(bf16[3,3072]{1,0:T(4,128)(2,1)S(1)} %pad_maximum_fusion.3), channel_id=1, source_target_pairs={{0,4},{4,8},{8,12},{1,5},{5,9},{9,13},{2,6},{6,10},{10,14},{3,7},{... | collective-permute-start | bytes 55304 | tf_op jit(solution)/shard_map/ppermute | solution.py:13
  25.5 1.6 copy-start.7
  25.5 2.3 copy-start
  26.9 10.6 %copy-start.6 = (f32[1,4,512]{2,1,0:T(4,128)S(1)}, f32[1,4,512]{2,1,0:T(4,128)}, u32[]{:S(2)}) copy-start(f32[1,4,512]{2,1,0:T(4,128)} %param.20) | copy-start | bytes 24580
  26.9 10.6 %copy-start.3 = (bf16[1,256,512]{2,1,0:T(8,128)(2,1)S(1)}, bf16[1,256,512]{2,1,0:T(8,128)(2,1)}, u32[]{:S(2)}) copy-start(bf16[1,256,512]{2,1,0:T(8,128)(2,1)} %param.15) | copy-start | bytes 786436
  27.0 118.6 %all-gather.5.cloned.1.call-start = ((), (), s32[]{:S(2)}) async-start(), calls=%async_computation.2 | async-start | bytes 5242880 | tf_op jit(solution)/shard_map/all_gather | solution.py:118
  80.0 3.0 %copy-start.1 = (f32[1,256,2048]{1,2,0:T(8,128)S(1)}, f32[1,256,2048]{1,2,0:T(8,128)}, u32[]{:S(2)}) copy-start(f32[1,256,2048]{1,2,0:T(8,128)} %copy.67) | copy-start | bytes 6291460
  80.0 3.0 %copy-start.4 = (f32[256,2,16]{0,2,1:T(8,128)S(1)}, f32[256,2,16]{0,2,1:T(8,128)}, u32[]{:S(2)}) copy-start(f32[256,2,16]{0,2,1:T(8,128)} %get-tuple-element.7) | copy-start | bytes 98308
  90.2 0.9 copy-start.5
  92.9 143.5 %reduce-scatter.2.cloned.1.call-start = ((), (), s32[]{:S(2)}) async-start(), calls=%async_computation.3 | async-start | bytes 5242880 | tf_op jit(solution)/shard_map/reduce_scatter | solution.py:124
  255.4 2.7 %collective-permute-start.1 = (bf16[64,8192]{1,0:T(8,128)(2,1)S(1)}, bf16[64,8192]{1,0:T(8,128)(2,1)S(1)}, u32[]{:S(2)}, u32[]{:S(2)}) collective-permute-start(bf16[64,8192]{1,0:T(8,128)(2,1)S(1)} %bitcast.104), channel_id=1, source_target_pairs={{16,0},{0,16},{17,1},{1,17},{18,2},{2,18},{19,3},{3,19},{20,4},{4,... | collective-permute-start | bytes 3145736 | tf_op jit(solution)/shard_map/ppermute | solution.py:30
Sparse Core Ops, SparseCore 0:
  27.1 52.8 all-gather.6
  93.0 52.5 all-gather.4
  159.6 76.7 reduce-scatter.1
where the time goes:
time: 266 us
  waiting for transfers between devices  174 us (65%)
  blocking collectives  25.7 us (10%)
  matrix products  22.9 us (9%)
  local copies, waits for them, and re-layouts  13.5 us (5%)
  between operations  13.4 us (5%)
  other arithmetic  11 us (4%)
  starting transfers between devices  5.03 us (2%)
    reduce_scatter x1, waiting for transfers between devices, per_device(): summed = lax.psum_scatter(terms, 'head', scatter_dimension=1, tiled=True)  77 us
    all_gather x1, waiting for transfers between devices, per_device(): lax.all_gather(hidden, 'seq', axis=0, tiled=True)  52.7 us
    all_gather x1, waiting for transfers between devices, entering(): blocks = lax.all_gather(block.astype(jnp.bfloat16), axis)  41.8 us
    all_to_all x1, blocking collectives, per_device(): lax.all_to_all(summed, 'seq', split_axis=0, concat_axis=2, tiled=True)  17.6 us
    dot_general x1, matrix products, per_device(): jnp.dot(lax.all_gather(hidden, 'seq', axis=0, tiled=True), local_weight,...  13.8 us
    all_gather x1, blocking collectives, entering(): decays = lax.all_gather(decay, axis)  8.08 us
  transfers between devices with their start and end apart: 5, of which 4 were waited for; matrix products, arithmetic and copies ran while one was open for 4% of the time, Pallas kernels for 0%

commit v1 on v0

--- a/solution.py
+++ b/solution.py
@@ -115,7 +115,9 @@
     hidden = ((gated * inverse_rms).reshape(length, x_cols) * norm_gain[0]).astype(jnp.bfloat16)
     local_weight = out_weight[0]
     terms = jnp.dot(
-        lax.all_gather(hidden, "seq", axis=0, tiled=True),
+        jnp.concatenate(
+            lax.all_to_all(jnp.stack([hidden] * lax.axis_size("seq")), "seq", 0, 0), axis=0
+        ),
         local_weight,
         preferred_element_type=jnp.float32,
     )

time: 266 us -> 268 us (level)
  waiting for transfers between devices: 174 us -> 120 us
  blocking collectives: 25.7 us -> 76.3 us
  local copies, waits for them, and re-layouts: 13.5 us -> 19.8 us
    all_gather x1 -> x0, waiting for transfers between devices: 52.7 us -> none  [per_device(): lax.all_gather(hidden, 'seq', axis=0, tiled=True)]
    all_to_all x0 -> x1, blocking collectives: none -> 50.7 us  [per_device(): lax.all_to_all(jnp.stack([hidden] * lax.axis_size('seq')), 'seq', 0, 0)]
    mul x1 -> x2, local copies, waits for them, and re-layouts: 0.61 us -> 5.99 us  [per_device(): gated * inverse_rms]
    dot_general x1, matrix products: 13.8 us -> 10.4 us  [per_device(): jnp.dot(jnp.concatenate(lax.all_to_all(jnp.stack([hidden] * lax.axis_size...]
  transfers between devices with their start and end apart: 5 -> 4, of which waited for: 4 -> 3; matrix products, arithmetic and copies ran while one was open for 4% -> 4% of each run, Pallas kernels for 0% -> 0%
where the time goes in v1:
time: 268 us; the launch traced here: 267 us
  waiting for transfers between devices  120 us (45%)
  blocking collectives  76.3 us (28%)
  matrix products  20.6 us (8%)
  local copies, waits for them, and re-layouts  19.8 us (7%)
  between operations  13.7 us (5%)
  other arithmetic  11.7 us (4%)
  starting transfers between devices  4.99 us (2%)
    reduce_scatter x1, waiting for transfers between devices, per_device(): summed = lax.psum_scatter(terms, 'head', scatter_dimension=1, tiled=True)  76.4 us
    all_to_all x1, blocking collectives, per_device(): lax.all_to_all(jnp.stack([hidden] * lax.axis_size('seq')), 'seq', 0, 0)  50.7 us
    all_gather x1, waiting for transfers between devices, entering(): blocks = lax.all_gather(block.astype(jnp.bfloat16), axis)  41.2 us
    all_to_all x1, blocking collectives, per_device(): lax.all_to_all(summed, 'seq', split_axis=0, concat_axis=2, tiled=True)  17.6 us
    dot_general x1, matrix products, per_device(): jnp.dot(jnp.concatenate(lax.all_to_all(jnp.stack([hidden] * lax.axis_size...  10.4 us
    all_gather x1, blocking collectives, entering(): decays = lax.all_gather(decay, axis)  8.09 us
    mul x2, local copies, waits for them, and re-layouts, per_device(): gated * inverse_rms  5.99 us
  transfers between devices with their start and end apart: 4, of which 3 were waited for; matrix products, arithmetic and copies ran while one was open for 4% of the time, Pallas kernels for 0%

profile of v1, /device:TPU:0, one launch (start us, length us, event | category | flops | bytes accessed | tf_op | source)
XLA Modules:
  0.0 267.4 jit_solution(13109016504884996876)
XLA Ops:
  6.5 0.9 slice_bitcast_fusion
  8.1 4.9 %collective-permute-start = (bf16[3,3072]{1,0:T(4,128)(2,1)S(1)}, bf16[3,3072]{1,0:T(4,128)(2,1)S(1)}, u32[]{:S(2)}, u32[]{:S(2)}) collective-permute-start(bf16[3,3072]{1,0:T(4,128)(2,1)S(1)} %pad_maximum_fusion.3), channel_id=1, source_target_pairs={{0,4},{4,8},{8,12},{1,5},{5,9},{9,13},{2,6},{6,10},{10,14},{3,7},{... | collective-permute-start | bytes 55304 | tf_op jit(solution)/shard_map/ppermute | solution.py:13
  14.2 1.3 reduce.9
  18.2 0.9 fusion.44
  19.2 1.4 multiply_bitcast_fusion
  20.6 0.9 fusion.47
  21.5 1.9 multiply_convert_fusion.6
  24.2 1.5 multiply_convert_fusion.3
  26.2 2.5 convolution_convert_fusion
  30.0 1.6 copy.67
  31.6 8.1 %all-gather = f32[8,16,1]{1,2,0:T(1,128)S(1)} all-gather(f32[2,16,1]{1,2,0:T(1,128)S(1)} %bitcast.106), channel_id=2, replica_groups=mesh['section'=2,'seq'=4,'head'=4] {'seq'}, dimensions={0}, use_global_device_ids=true | all-gather | bytes 640 | tf_op jit(solution)/shard_map/all_gather | solution.py:18
  40.5 41.2 %all-gather.4.cloned.1.call-done = bf16[8,16,64,256]{3,2,1,0:T(8,128)(2,1)} async-done(((bf16[2,16,64,256]{3,2,1,0:T(8,128)(2,1)}), bf16[8,16,64,256]{3,2,1,0:T(8,128)(2,1)}) %all-gather.4.cloned.1.call-update) | async-done | bytes 4194320 | tf_op jit(solution)/shard_map/all_gather | solution.py:19
  81.7 3.0 %fusion.24 = f32[2,16,64,256]{3,2,1,0:T(8,128)S(1)} fusion(bf16[8,16,64,256]{3,2,1,0:T(8,128)(2,1)} %all-gather.4.cloned.1.call-done, f32[2,16]{1,0:T(2,128)S(1)} %bitcast.109, f32[2,16]{1,0:T(2,128)S(1)} %bitcast.108, f32[2,16]{1,0:T(2,128)S(1)} %bitcast.107, pred[]{:T(512)S(6)} %gt.11, pred[]{:T(512)S(6)} %gt.10, pred[]{:T(512)S(6)} %gt.9, ...), kind=kOutput, calls=%fused_computation.35 | convolution fusion | flops 274726912 | bytes 5505411 | tf_op jit(solution)/shard_map/tgn,gjpn->tgjp/dot_general | solution.py:106
  84.7 4.5 %multiply_reduce_fusion = (f32[256,2]{0,1:T(2,128)S(1)}, f32[256,2,16,64]{0,3,2,1:T(8,128)}) fusion(f32[256,2,16,64]{0,3,2,1:T(8,128)S(1)} %bitcast.80, bf16[256,2,16,64]{0,3,2,1:T(8,128)(2,1)S(1)} %bitcast.84, f32[2,16]{1,0:T(2,128)S(1)} %copy-done.8, f32[256,2,16]{0,2,1:T(8,128)S(1)} %copy-done.4, f32[2,16,64,256]{3,2,1,0:T(8,128)S(1)} %fusion.24, ...), kind=kOutput, calls=%fused_computation.26 | convolution fusion | flops 287309312 | bytes 8030336 | tf_op jit(solution)/shard_map/gjtu,ugjp->tgjp/dot_general | solution.py:95
  89.2 1.9 copy.66
  91.3 2.0 mul.328
  93.3 4.0 %mul.329 = f32[1,256,2048]{2,1,0:T(8,128)} reshape(f32[256,2,1024]{2,1,0:T(2,128)} %mul.328) | data formatting | bytes 4194304 | tf_op jit(solution)/shard_map/mul | solution.py:115
  97.3 2.5 fusion.29
  100.3 50.7 %all_to_all.20 = bf16[4,256,2048]{2,1,0:T(8,128)(2,1)S(1)} all-to-all(bf16[4,256,2048]{2,1,0:T(8,128)(2,1)S(1)} %stack.10), channel_id=1, replica_groups=mesh['section'=2,'seq'=4,'head'=4] {'seq'}, dimensions={0} | all-to-all | bytes 8388608 | tf_op jit(solution)/shard_map/all_to_all | solution.py:119
  151.0 10.4 %fusion.9 = bf16[1024,2048]{1,0:T(8,128)(2,1)} fusion(bf16[1024,2048]{1,0:T(8,128)(2,1)S(1)} %bitcast.75, bf16[1,2048,2048]{2,1,0:T(8,128)(2,1)S(1)} %bitcast.112), kind=kOutput, calls=%fused_computation.10 | convolution fusion | flops 8592031744 | bytes 16777216 | tf_op jit(solution)/shard_map/dot_general | solution.py:117
  161.4 76.4 %reduce-scatter.2.cloned.1.call-done = bf16[4,64,2048]{2,1,0:T(8,128)(2,1)} async-done(((bf16[4,256,2048]{2,1,0:T(8,128)(2,1)}), bf16[4,64,2048]{2,1,0:T(8,128)(2,1)}) %reduce-scatter.2.cloned.1.call-update) | async-done | bytes 1048592 | tf_op jit(solution)/shard_map/reduce_scatter | solution.py:126
  237.8 17.6 %all_to_all.21 = bf16[4,64,2048]{2,1,0:T(8,128)(2,1)S(1)} all-to-all(bf16[4,64,2048]{2,1,0:T(8,128)(2,1)} %reduce-scatter.2.cloned.1.call-done), channel_id=1, replica_groups=mesh['section'=2,'seq'=4,'head'=4] {'seq'}, dimensions={0} | all-to-all | bytes 2097152 | tf_op jit(solution)/shard_map/all_to_all | solution.py:127
  256.9 2.6 collective-permute-done.1
  259.6 1.0 copy.96
  (63 shorter events, 10.2 us)
Async XLA Ops:
  6.5 17.6 %copy-start.2 = (bf16[1,256,2048]{2,1,0:T(8,128)(2,1)S(1)}, bf16[1,256,2048]{2,1,0:T(8,128)(2,1)}, u32[]{:S(2)}) copy-start(bf16[1,256,2048]{2,1,0:T(8,128)(2,1)} %param.13) | copy-start | bytes 3145732
  6.5 75.2 %all-gather.4.cloned.1.call-start = ((), (), s32[]{:S(2)}) async-start(), calls=%async_computation.4 | async-start | bytes 5242880 | tf_op jit(solution)/shard_map/all_gather | solution.py:19
  8.1 13.3 %collective-permute-start = (bf16[3,3072]{1,0:T(4,128)(2,1)S(1)}, bf16[3,3072]{1,0:T(4,128)(2,1)S(1)}, u32[]{:S(2)}, u32[]{:S(2)}) collective-permute-start(bf16[3,3072]{1,0:T(4,128)(2,1)S(1)} %pad_maximum_fusion.3), channel_id=1, source_target_pairs={{0,4},{4,8},{8,12},{1,5},{5,9},{9,13},{2,6},{6,10},{10,14},{3,7},{... | collective-permute-start | bytes 55304 | tf_op jit(solution)/shard_map/ppermute | solution.py:13
  26.2 2.6 copy-start.7
  26.2 3.8 %copy-start = (bf16[1,256,2048]{2,1,0:T(8,128)(2,1)S(1)}, bf16[1,256,2048]{2,1,0:T(8,128)(2,1)}, u32[]{:S(2)}) copy-start(bf16[1,256,2048]{2,1,0:T(8,128)(2,1)} %param.16) | copy-start | bytes 3145732
  28.7 11.1 %copy-start.6 = (f32[1,4,512]{2,1,0:T(4,128)S(1)}, f32[1,4,512]{2,1,0:T(4,128)}, u32[]{:S(2)}) copy-start(f32[1,4,512]{2,1,0:T(4,128)} %param.20) | copy-start | bytes 24580
  28.7 11.1 %copy-start.3 = (bf16[1,256,512]{2,1,0:T(8,128)(2,1)S(1)}, bf16[1,256,512]{2,1,0:T(8,128)(2,1)}, u32[]{:S(2)}) copy-start(bf16[1,256,512]{2,1,0:T(8,128)(2,1)} %param.15) | copy-start | bytes 786436
  28.7 209.1 %reduce-scatter.2.cloned.1.call-start = ((), (), s32[]{:S(2)}) async-start(), calls=%async_computation.3 | async-start | bytes 5242880 | tf_op jit(solution)/shard_map/reduce_scatter | solution.py:126
  81.7 3.0 %copy-start.1 = (f32[1,256,2048]{1,2,0:T(8,128)S(1)}, f32[1,256,2048]{1,2,0:T(8,128)}, u32[]{:S(2)}) copy-start(f32[1,256,2048]{1,2,0:T(8,128)} %copy.67) | copy-start | bytes 6291460
  81.7 3.0 %copy-start.4 = (f32[256,2,16]{0,2,1:T(8,128)S(1)}, f32[256,2,16]{0,2,1:T(8,128)}, u32[]{:S(2)}) copy-start(f32[256,2,16]{0,2,1:T(8,128)} %get-tuple-element.7) | copy-start | bytes 98308
  81.7 3.0 %copy-start.8 = (f32[2,16]{1,0:T(2,128)S(1)}, f32[2,16]{1,0:T(2,128)}, u32[]{:S(2)}) copy-start(f32[2,16]{1,0:T(2,128)} %mul.320) | copy-start | bytes 388
  93.3 4.0 %copy-start.5 = (f32[1,2048]{1,0:T(1,128)S(1)}, f32[1,2048]{1,0:T(1,128)}, u32[]{:S(2)}) copy-start(f32[1,2048]{1,0:T(1,128)} %param.24) | copy-start | bytes 24580
  97.3 53.7 %slice-start = ((s8[8388608]{0:T(1024)(128)(4,1)}), s8[4194304]{0:T(1024)(128)(4,1)S(1)}, s32[]{:S(2)}) async-start(s8[8388608]{0:T(1024)(128)(4,1)} %bitcast.111), calls=%async_computation.5 | async-start | bytes 8388608
  99.8 51.2 %slice-start.1 = ((s8[8388608]{0:T(1024)(128)(4,1)}), s8[4194304]{0:T(1024)(128)(4,1)S(1)}, s32[]{:S(2)}) async-start(s8[8388608]{0:T(1024)(128)(4,1)} %bitcast.111), calls=%async_computation.6 | async-start | bytes 8388608
  256.9 2.7 %collective-permute-start.1 = (bf16[64,8192]{1,0:T(8,128)(2,1)S(1)}, bf16[64,8192]{1,0:T(8,128)(2,1)S(1)}, u32[]{:S(2)}, u32[]{:S(2)}) collective-permute-start(bf16[64,8192]{1,0:T(8,128)(2,1)S(1)} %bitcast.85), channel_id=1, source_target_pairs={{16,0},{0,16},{17,1},{1,17},{18,2},{2,18},{19,3},{3,19},{20,4},{4,... | collective-permute-start | bytes 3145736 | tf_op jit(solution)/shard_map/ppermute | solution.py:30
Sparse Core Ops, SparseCore 0:
  28.8 52.8 all-gather.3
  161.6 76.2 reduce-scatter.1
